TPU v7x, 128 devices: a whole 4x4x4 slice. The times are simulated.
128 devices in a mesh: dp: 8 (over z, core), mp: 16 (over y, x).
Axes of the slice: x: 4, y: 4, z: 4, core: 2. Of those that a mesh axis runs over, the one named last changes fastest.
Arguments:
- crop_hidden: bfloat16 [8, 1536, 8192], P(None, 'dp', 'mp'), may hold values from -15 to 15
- projector_weight: bfloat16 [8192, 8192], P('mp'), may hold values from -0.21213203 to 0.21213203
- pairing: int32 [8, 1536], P(None, 'dp'), may hold values from 0 to 191, as said below
Outputs:
- embeddings: float32 [8192, 8, 1536], P('mp', 'dp')
- loss_terms: float32 [4], replicated
Inputs may be any that keep to these rules, and one draw needn't show every extreme that they name: Each aligned block of 192 entries of a row of pairing is a permutation of 0 to 191.
All inputs are finite; a program needn't handle non-finite values.
Results may differ from a plain program's by a relative error of at most 0.0003.
Values may be sent and summed in bfloat16 or wider, within the bound.
No kernel may reach another device: no remote copies, remote signals or barrier semaphores. Data moves between devices by JAX's collectives and lax.ppermute only.
A program may use at most 128 MiB of HBM per device.

v0:
```python
import functools
import jax
import jax.numpy as jnp
from jax import lax
from jax.sharding import Mesh
from jax.sharding import PartitionSpec as P

MP = ("mp_0", "mp_1")
DP = ("dp_0", "dp_1")
DP_MP = ("dp_0", "dp_1", "mp_0", "mp_1")
highest = lax.Precision.HIGHEST
epsilon = 0.0001


def by_axis(x, axes):
    return functools.reduce(lax.psum, axes, x)


def local(crop_hidden, projector_weight, pairing):
    crop_count, local_rows, width_part = crop_hidden.shape
    features = projector_weight.shape[1]
    total_rows = crop_count * local_rows
    column_block = lax.all_to_all(projector_weight, MP, split_axis=1, concat_axis=0, tiled=True)
    shards = lax.all_gather(crop_hidden, MP, axis=2, tiled=True)
    flat_piece = shards.reshape(total_rows, shards.shape[2])
    embedded = lax.dot_general(
        column_block, flat_piece, (((0,), (1,)), ((), ())), preferred_element_type=jnp.float32
    )
    feature_part = embedded.shape[0]
    by_crop = embedded.reshape(feature_part, crop_count, local_rows)
    onehot = (pairing[:, :, None] == jnp.arange(local_rows, dtype=jnp.int32)[None, None, :]).astype(
        jnp.float32
    )
    aligned = jnp.einsum("jcr,cri->jci", by_crop, onehot, precision=highest)
    invariance = 0.0
    for anchor in range(2):
        differ = aligned - aligned[:, anchor : anchor + 1, :]
        invariance = invariance + jnp.sum(differ * differ)
    owned_block = lax.all_to_all(by_crop, DP, split_axis=1, concat_axis=2, tiled=True)
    batch_rows = owned_block.shape[2]
    column_mean = jnp.mean(owned_block, axis=2, keepdims=True)
    centered = owned_block - column_mean
    variance = jnp.sum(centered * centered, axis=2) / (batch_rows - 1)
    hinge_sum = jnp.sum(jax.nn.relu(1.0 - jnp.sqrt(variance + epsilon)))
    diagonal_sq = jnp.sum(variance * variance)
    gram_scale = 1.0 / ((batch_rows - 1) * (batch_rows - 1))
    partial_gram = jnp.einsum("jcr,jcs->crs", centered, centered, precision=highest)
    gram_block = lax.psum(partial_gram.astype(jnp.bfloat16), MP).astype(jnp.float32)
    frobenius = jnp.where(
        lax.axis_index(MP) == 0, jnp.sum(gram_block * gram_block) * gram_scale, 0.0
    )
    totals = (
        by_axis(invariance, DP_MP),
        by_axis(hinge_sum, DP_MP),
        by_axis(frobenius - diagonal_sq, DP_MP),
    )
    invariance_loss = totals[0] / (2 * (crop_count - 1) * batch_rows * features)
    variance_loss = totals[1] / (crop_count * features)
    covariance_loss = totals[2] / (crop_count * features)
    total_loss = 25.0 * invariance_loss + 25.0 * variance_loss + covariance_loss
    loss_terms = jnp.stack([invariance_loss, variance_loss, covariance_loss, total_loss])
    return (owned_block, loss_terms)


def solution(mesh):
    torus = Mesh(mesh.devices.reshape(4, 2, 4, 4), ("dp_0", "dp_1", "mp_0", "mp_1"))
    placed = (P(None, DP, MP), P(MP, None), P(None, DP))
    return jax.shard_map(
        local, mesh=torus, in_specs=placed, out_specs=(P(MP, DP, None), P()), check_vma=False
    )
```

profile of v0, /device:TPU:0, one launch (start us, length us, event | category | flops | bytes accessed | tf_op | source)
XLA Modules:
  0.0 498.9 jit_solution(17605152332946094416)
XLA Ops:
  7.2 0.0 all-gather.2.cloned.1.call-start
  7.2 0.7 all-gather.2.cloned.1.call-update
  7.9 0.0 all-reduce.6.cloned.1.call-start
  7.9 7.5 %copy.9 = bf16[64,16,8,512]{3,2,0,1:T(8,128)(2,1)} copy(bf16[64,16,8,512]{3,2,1,0:T(8,128)(2,1)} %bitcast.30) | data formatting | bytes 16777216 | tf_op jit(solution)/shard_map/all_to_all | solution.py:23
  15.4 128.3 %all_to_all.31 = bf16[512,16,512]{2,0,1:T(8,128)(2,1)} all-to-all(bf16[512,16,512]{2,0,1:T(8,128)(2,1)} %bitcast.29), channel_id=1, replica_groups=mesh['dp_0'=4,'dp_1'=2,'mp_0'=4,'mp_1'=4] {'mp_0','mp_1'}, dimensions={1} | all-to-all | bytes 16777216 | tf_op jit(solution)/shard_map/all_to_all | solution.py:23
  143.8 117.0 %all-gather.2.cloned.1.call-done = bf16[8,192,8192]{2,1,0:T(8,128)(2,1)} async-done(((bf16[8,192,512]{2,1,0:T(8,128)(2,1)}), bf16[8,192,8192]{2,1,0:T(8,128)(2,1)}) %all-gather.2.cloned.1.call-update) | async-done | bytes 25165840 | tf_op jit(solution)/shard_map/all_gather | solution.py:24
  260.8 18.9 %fusion.2 = f32[512,8,192]{0,2,1:T(8,128)S(1)} fusion(bf16[8192,512,1]{1,0,2:T(8,128)(2,1)} %bitcast.31, bf16[8,192,8192]{2,1,0:T(8,128)(2,1)} %all-gather.2.cloned.1.call-done), kind=kOutput, calls=%fused_computation.17 | convolution fusion | flops 12884901888 | bytes 36700160 | tf_op jit(solution)/shard_map/dot_general | solution.py:26
  279.7 0.0 copy-start
  279.7 1.7 copy-done
  281.3 42.7 %all_to_all.32 = f32[512,8,192]{0,2,1:T(8,128)S(1)} all-to-all(f32[512,8,192]{0,2,1:T(8,128)S(1)} %fusion.2), channel_id=1, replica_groups=mesh['dp_0'=4,'dp_1'=2,'mp_0'=4,'mp_1'=4] {'dp_0','dp_1'}, dimensions={1} | all-to-all | bytes 6291456 | tf_op jit(solution)/shard_map/all_to_all | solution.py:39
  324.0 0.3 reduce_sum.65
  324.3 0.6 multiply_reduce_fusion.1
  324.8 16.8 %fusion = bf16[1,1536,1536]{2,1,0:T(8,128)(2,1)} fusion(f32[512,1536]{0,1:T(8,128)S(1)} %bitcast.32), kind=kOutput, calls=%fused_computation.3 | convolution fusion | flops 14497873920 | bytes 7864320 | tf_op jit(solution)/shard_map/jcr,jcs->crs/dot_general | solution.py:47
  341.6 0.0 copy-start.1
  341.6 0.0 all-reduce.6.cloned.1.call-update
  341.6 0.7 copy-done.1
  342.3 3.9 convolution_bitcast_fusion
  346.2 0.1 slice_bitcast_fusion.1
  346.2 2.0 multiply_reduce_fusion.2
  349.5 5.4 %copy.6 = f32[512,1,1536]{2,1,0:T(1,128)} copy(f32[512,1,1536]{0,2,1:T(8,128)S(1)} %bitcast.28) | data formatting | bytes 6291456
  354.9 0.7 multiply_reduce_fusion.4
  355.6 91.4 %all-reduce.6.cloned.1.call-done = bf16[1,1536,1536]{2,1,0:T(8,128)(2,1)} async-done(((bf16[1,1536,1536]{2,1,0:T(8,128)(2,1)}), bf16[1,1536,1536]{2,1,0:T(8,128)(2,1)}) %all-reduce.6.cloned.1.call-update) | async-done | bytes 4718608 | tf_op jit(solution)/shard_map/psum | solution.py:48
  447.0 5.3 %multiply_reduce_fusion = f32[]{:T(128)} fusion(bf16[1,1536,1536]{2,1,0:T(8,128)(2,1)} %all-reduce.6.cloned.1.call-done), kind=kLoop, calls=%fused_computation | loop fusion | flops 7077887 | bytes 4718596 | tf_op jit(solution)/shard_map/reduce_sum | solution.py:50
  453.5 11.3 %all-reduce.2 = (f32[]{:T(128)}, f32[]{:T(128)}, f32[]{:T(128)}) all-reduce(f32[]{:T(128)S(6)} %add.47, f32[]{:T(128)} %get-tuple-element.7, f32[]{:T(128)S(6)} %sub.61), channel_id=1, replica_groups=mesh['dp_0'=4,'dp_1'=2,'mp_0'=4,'mp_1'=4] {'dp_0'}, use_global_device_ids=true, to_apply=%region_2.0 | all-reduce | flops 3 | bytes 24 | tf_op jit(solution)/shard_map/psum | solution.py:16
  464.8 3.2 all-reduce.3
  467.9 11.0 %all-reduce.1 = (f32[]{:T(128)}, f32[]{:T(128)}, f32[]{:T(128)}) all-reduce(f32[]{:T(128)} %get-tuple-element.17, f32[]{:T(128)} %get-tuple-element.18, f32[]{:T(128)} %get-tuple-element.19), channel_id=1, replica_groups=mesh['dp_0'=4,'dp_1'=2,'mp_0'=4,'mp_1'=4] {'mp_0'}, use_global_device_ids=true, to_apply=%region_4.5 | all-reduce | flops 3 | bytes 24 | tf_op jit(solution)/shard_map/psum | solution.py:16
  478.9 9.4 %all-reduce = (f32[]{:T(128)}, f32[]{:T(128)}, f32[]{:T(128)}) all-reduce(f32[]{:T(128)} %get-tuple-element.11, f32[]{:T(128)} %get-tuple-element.12, f32[]{:T(128)} %get-tuple-element.13), channel_id=1, replica_groups=mesh['dp_0'=4,'dp_1'=2,'mp_0'=4,'mp_1'=4] {'mp_1'}, use_global_device_ids=true, to_apply=%region_5.6 | all-reduce | flops 3 | bytes 24 | tf_op jit(solution)/shard_map/psum | solution.py:16
  491.5 0.6 pad_maximum_fusion
  (1 shorter events, 0.0 us)
Async XLA Ops:
  7.2 253.6 %all-gather.2.cloned.1.call-start = ((), (), s32[]{:S(2)}) async-start(), calls=%async_computation.2 | async-start | bytes 26738688 | tf_op jit(solution)/shard_map/all_gather | solution.py:24
  7.9 439.1 %all-reduce.6.cloned.1.call-start = ((), (), s32[]{:S(2)}) async-start(), calls=%async_computation.3 | async-start | bytes 9437184 | tf_op jit(solution)/shard_map/psum | solution.py:48
  279.7 1.7 copy-start
  341.6 0.7 copy-start.1
Sparse Core Ops, SparseCore 0:
  10.1 250.6 all-gather.1
  341.7 105.2 all-reduce.5
where the time goes:
time: 499 us
  waiting for transfers between devices  209 us (42%)
  blocking collectives  206 us (41%)
  matrix products  39.5 us (8%)
  between operations  19.8 us (4%)
  local copies, waits for them, and re-layouts  15.3 us (3%)
  other arithmetic  9.4 us (2%)
    all_to_all x1, blocking collectives, local(): lax.all_to_all(projector_weight, MP, split_axis=1, concat_axis=0, tiled=T...  128 us
    all_gather x1, waiting for transfers between devices, local(): shards = lax.all_gather(crop_hidden, MP, axis=2, tiled=True)  117 us
    psum x1, waiting for transfers between devices, local(): lax.psum(partial_gram.astype(jnp.bfloat16), MP).astype(jnp.float32)  91.4 us
    all_to_all x1, blocking collectives, local(): lax.all_to_all(by_crop, DP, split_axis=1, concat_axis=2, tiled=True)  42.7 us
    psum x4, blocking collectives, by_axis(): return functools.reduce(lax.psum, axes, x)  34.8 us
    dot_general x1, matrix products, local(): lax.dot_general(column_block, flat_piece, (((0,), (1,)), ((), ())), prefe...  18.9 us
    dot_general x1, matrix products, local(): jnp.einsum('jcr,jcs->crs', centered, centered, precision=highest)  16.8 us
  transfers between devices with their start and end apart: 2, of which 2 were waited for; matrix products, arithmetic and copies ran while one was open for 4% of the time, Pallas kernels for 0%

commit v1 on v0

--- a/solution.py
+++ b/solution.py
@@ -45,7 +45,9 @@
     diagonal_sq = jnp.sum(variance * variance)
     gram_scale = 1.0 / ((batch_rows - 1) * (batch_rows - 1))
     partial_gram = jnp.einsum("jcr,jcs->crs", centered, centered, precision=highest)
-    gram_block = lax.psum(partial_gram.astype(jnp.bfloat16), MP).astype(jnp.float32)
+    gram_block = lax.psum(lax.psum(partial_gram.astype(jnp.bfloat16), "mp_1"), "mp_0").astype(
+        jnp.float32
+    )
     frobenius = jnp.where(
         lax.axis_index(MP) == 0, jnp.sum(gram_block * gram_block) * gram_scale, 0.0
     )

time: 499 us -> 596 us (1.19)
  waiting for transfers between devices: 209 us -> 307 us
    psum x1 -> x2, waiting for transfers between devices: 91.4 us -> 189 us  [the longest x1 98.6 us: local(): lax.psum(partial_gram.astype(jnp.bfloat16), 'mp_1')]
  transfers between devices with their start and end apart: 2 -> 3, of which waited for: 2 -> 3; matrix products, arithmetic and copies ran while one was open for 4% -> 3% of each run, Pallas kernels for 0% -> 0%
where the time goes in v1:
time: 596 us
  waiting for transfers between devices  307 us (52%)
  blocking collectives  206 us (35%)
  matrix products  39.5 us (7%)
  between operations  19.7 us (3%)
  local copies, waits for them, and re-layouts  14.6 us (2%)
  other arithmetic  9.51 us (2%)
    all_to_all x1, blocking collectives, local(): lax.all_to_all(projector_weight, MP, split_axis=1, concat_axis=0, tiled=T...  128 us
    all_gather x1, waiting for transfers between devices, local(): shards = lax.all_gather(crop_hidden, MP, axis=2, tiled=True)  117 us
    psum x1, waiting for transfers between devices, local(): lax.psum(partial_gram.astype(jnp.bfloat16), 'mp_1')  98.6 us
    psum x1, waiting for transfers between devices, local(): lax.psum(lax.psum(partial_gram.astype(jnp.bfloat16), 'mp_1'), 'mp_0')  90.2 us
    all_to_all x1, blocking collectives, local(): lax.all_to_all(by_crop, DP, split_axis=1, concat_axis=2, tiled=True)  42.7 us
    psum x4, blocking collectives, by_axis(): return functools.reduce(lax.psum, axes, x)  34.8 us
    dot_general x1, matrix products, local(): lax.dot_general(column_block, flat_piece, (((0,), (1,)), ((), ())), prefe...  18.9 us
    dot_general x1, matrix products, local(): jnp.einsum('jcr,jcs->crs', centered, centered, precision=highest)  16.8 us
  transfers between devices with their start and end apart: 3, of which 3 were waited for; matrix products, arithmetic and copies ran while one was open for 3% of the time, Pallas kernels for 0%

profile of v1, /device:TPU:0, one launch (start us, length us, event | category | flops | bytes accessed | tf_op | source)
XLA Modules:
  0.0 595.9 jit_solution(983775859717368523)
XLA Ops:
  7.2 0.0 all-gather.2.cloned.1.call-start
  7.2 0.7 all-gather.2.cloned.1.call-update
  7.9 0.0 all-reduce.7.cloned.1.call-start
  7.9 7.5 %copy.9 = bf16[64,16,8,512]{3,2,0,1:T(8,128)(2,1)} copy(bf16[64,16,8,512]{3,2,1,0:T(8,128)(2,1)} %bitcast.30) | data formatting | bytes 16777216 | tf_op jit(solution)/shard_map/all_to_all | solution.py:23
  15.4 128.3 %all_to_all.31 = bf16[512,16,512]{2,0,1:T(8,128)(2,1)} all-to-all(bf16[512,16,512]{2,0,1:T(8,128)(2,1)} %bitcast.29), channel_id=1, replica_groups=mesh['dp_0'=4,'dp_1'=2,'mp_0'=4,'mp_1'=4] {'mp_0','mp_1'}, dimensions={1} | all-to-all | bytes 16777216 | tf_op jit(solution)/shard_map/all_to_all | solution.py:23
  143.8 117.0 %all-gather.2.cloned.1.call-done = bf16[8,192,8192]{2,1,0:T(8,128)(2,1)} async-done(((bf16[8,192,512]{2,1,0:T(8,128)(2,1)}), bf16[8,192,8192]{2,1,0:T(8,128)(2,1)}) %all-gather.2.cloned.1.call-update) | async-done | bytes 25165840 | tf_op jit(solution)/shard_map/all_gather | solution.py:24
  260.8 18.9 %fusion.2 = f32[512,8,192]{0,2,1:T(8,128)S(1)} fusion(bf16[8192,512,1]{1,0,2:T(8,128)(2,1)} %bitcast.31, bf16[8,192,8192]{2,1,0:T(8,128)(2,1)} %all-gather.2.cloned.1.call-done), kind=kOutput, calls=%fused_computation.17 | convolution fusion | flops 12884901888 | bytes 36700160 | tf_op jit(solution)/shard_map/dot_general | solution.py:26
  279.7 0.0 copy-start
  279.7 1.7 copy-done
  281.3 42.7 %all_to_all.32 = f32[512,8,192]{0,2,1:T(8,128)S(1)} all-to-all(f32[512,8,192]{0,2,1:T(8,128)S(1)} %fusion.2), channel_id=1, replica_groups=mesh['dp_0'=4,'dp_1'=2,'mp_0'=4,'mp_1'=4] {'dp_0','dp_1'}, dimensions={1} | all-to-all | bytes 6291456 | tf_op jit(solution)/shard_map/all_to_all | solution.py:39
  324.0 0.3 reduce_sum.65
  324.3 0.6 multiply_reduce_fusion.1
  324.8 16.8 %fusion = bf16[1,1536,1536]{2,1,0:T(8,128)(2,1)} fusion(f32[512,1536]{0,1:T(8,128)S(1)} %bitcast.32), kind=kOutput, calls=%fused_computation.3 | convolution fusion | flops 14497873920 | bytes 7864320 | tf_op jit(solution)/shard_map/jcr,jcs->crs/dot_general | solution.py:47
  341.6 0.0 all-reduce.7.cloned.1.call-update
  341.6 0.0 copy-start.1
  341.6 0.2 all-reduce.9.cloned.1.call-start
  341.8 98.6 %all-reduce.7.cloned.1.call-done = bf16[1,1536,1536]{2,1,0:T(8,128)(2,1)} async-done(((bf16[1,1536,1536]{2,1,0:T(8,128)(2,1)}), bf16[1,1536,1536]{2,1,0:T(8,128)(2,1)}) %all-reduce.7.cloned.1.call-update) | async-done | bytes 4718608 | tf_op jit(solution)/shard_map/psum | solution.py:48
  440.4 0.0 all-reduce.9.cloned.1.call-update
  440.4 0.0 copy-done.1
  440.4 3.9 convolution_bitcast_fusion
  444.3 0.1 slice_bitcast_fusion.1
  444.4 2.0 multiply_reduce_fusion.2
  447.7 5.4 copy.6
  453.1 0.7 multiply_reduce_fusion.4
  453.8 90.2 %all-reduce.9.cloned.1.call-done = bf16[1,1536,1536]{2,1,0:T(8,128)(2,1)} async-done(((bf16[1,1536,1536]{2,1,0:T(8,128)(2,1)}), bf16[1,1536,1536]{2,1,0:T(8,128)(2,1)}) %all-reduce.9.cloned.1.call-update) | async-done | bytes 4718608 | tf_op jit(solution)/shard_map/psum | solution.py:48
  544.0 5.4 multiply_reduce_fusion
  550.8 11.3 %all-reduce.2 = (f32[]{:T(128)}, f32[]{:T(128)}, f32[]{:T(128)}) all-reduce(f32[]{:T(128)S(6)} %add.49, f32[]{:T(128)} %get-tuple-element.7, f32[]{:T(128)S(6)} %sub.61), channel_id=1, replica_groups=mesh['dp_0'=4,'dp_1'=2,'mp_0'=4,'mp_1'=4] {'dp_0'}, use_global_device_ids=true, to_apply=%region_2.0 | all-reduce | flops 3 | bytes 24 | tf_op jit(solution)/shard_map/psum | solution.py:16
  562.0 3.2 all-reduce.3
  565.2 9.2 %all-reduce.1 = (f32[]{:T(128)}, f32[]{:T(128)}, f32[]{:T(128)}) all-reduce(f32[]{:T(128)} %get-tuple-element.17, f32[]{:T(128)} %get-tuple-element.18, f32[]{:T(128)} %get-tuple-element.19), channel_id=1, replica_groups=mesh['dp_0'=4,'dp_1'=2,'mp_0'=4,'mp_1'=4] {'mp_0'}, use_global_device_ids=true, to_apply=%region_4.5 | all-reduce | flops 3 | bytes 24 | tf_op jit(solution)/shard_map/psum | solution.py:16
  574.5 11.1 %all-reduce = (f32[]{:T(128)}, f32[]{:T(128)}, f32[]{:T(128)}) all-reduce(f32[]{:T(128)} %get-tuple-element.11, f32[]{:T(128)} %get-tuple-element.12, f32[]{:T(128)} %get-tuple-element.13), channel_id=1, replica_groups=mesh['dp_0'=4,'dp_1'=2,'mp_0'=4,'mp_1'=4] {'mp_1'}, use_global_device_ids=true, to_apply=%region_5.6 | all-reduce | flops 3 | bytes 24 | tf_op jit(solution)/shard_map/psum | solution.py:16
  588.8 0.6 pad_maximum_fusion
  (1 shorter events, 0.0 us)
Async XLA Ops:
  7.2 253.6 %all-gather.2.cloned.1.call-start = ((), (), s32[]{:S(2)}) async-start(), calls=%async_computation.2 | async-start | bytes 26738688 | tf_op jit(solution)/shard_map/all_gather | solution.py:24
  7.9 432.5 %all-reduce.7.cloned.1.call-start = ((), (), s32[]{:S(2)}) async-start(), calls=%async_computation.3 | async-start | bytes 9437184 | tf_op jit(solution)/shard_map/psum | solution.py:48
  279.7 1.7 copy-start
  341.6 98.8 %copy-start.1 = (s32[8,192]{1,0:T(8,128)S(1)}, s32[8,192]{1,0:T(8,128)}, u32[]{:S(2)}) copy-start(s32[8,192]{1,0:T(8,128)} %param.5) | copy-start | bytes 18436
  341.6 202.4 %all-reduce.9.cloned.1.call-start = ((), (), s32[]{:S(2)}) async-start(), calls=%async_computation.4 | async-start | bytes 9437184 | tf_op jit(solution)/shard_map/psum | solution.py:48
Sparse Core Ops, SparseCore 0:
  10.1 250.6 all-gather.1
  341.7 98.6 all-reduce.6
  442.8 101.1 all-reduce.8

commit v2 on v0

--- a/solution.py
+++ b/solution.py
@@ -21,7 +21,7 @@
     features = projector_weight.shape[1]
     total_rows = crop_count * local_rows
     column_block = lax.all_to_all(projector_weight, MP, split_axis=1, concat_axis=0, tiled=True)
-    shards = lax.all_gather(crop_hidden, MP, axis=2, tiled=True)
+    shards = jnp.concatenate(lax.all_gather(crop_hidden, MP), axis=2)
     flat_piece = shards.reshape(total_rows, shards.shape[2])
     embedded = lax.dot_general(
         column_block, flat_piece, (((0,), (1,)), ((), ())), preferred_element_type=jnp.float32

time: 499 us -> 486 us (0.974)
  local copies, waits for them, and re-layouts: 15.3 us -> 32.2 us
  waiting for transfers between devices: 209 us -> 193 us
  blocking collectives: 206 us -> 191 us
    all_gather x1, waiting for transfers between devices: 117 us -> 101 us  [local(): shards = jnp.concatenate(lax.all_gather(crop_hidden, MP), axis=2)]
    all_to_all x1, blocking collectives: 128 us -> 114 us  [local(): lax.all_to_all(projector_weight, MP, split_axis=1, concat_axis=0, tiled=T...]
    unnamed x5 -> x6, local copies, waits for them, and re-layouts: 7.75 us -> 19.7 us
  transfers between devices with their start and end apart: 2 -> 2, of which waited for: 2 -> 2; matrix products, arithmetic and copies ran while one was open for 4% -> 8% of each run, Pallas kernels for 0% -> 0%
where the time goes in v2:
time: 486 us; the launch traced here: 485 us
  waiting for transfers between devices  193 us (40%)
  blocking collectives  191 us (39%)
  matrix products  39.5 us (8%)
  local copies, waits for them, and re-layouts  32.2 us (7%)
  between operations  19.8 us (4%)
  other arithmetic  9.4 us (2%)
    all_to_all x1, blocking collectives, local(): lax.all_to_all(projector_weight, MP, split_axis=1, concat_axis=0, tiled=T...  114 us
    all_gather x1, waiting for transfers between devices, local(): shards = jnp.concatenate(lax.all_gather(crop_hidden, MP), axis=2)  101 us
    psum x1, waiting for transfers between devices, local(): lax.psum(partial_gram.astype(jnp.bfloat16), MP).astype(jnp.float32)  91.3 us
    all_to_all x1, blocking collectives, local(): lax.all_to_all(by_crop, DP, split_axis=1, concat_axis=2, tiled=True)  42.6 us
    psum x4, blocking collectives, by_axis(): return functools.reduce(lax.psum, axes, x)  34.8 us
    unnamed x6, local copies, waits for them, and re-layouts  19.7 us
    dot_general x1, matrix products, local(): lax.dot_general(column_block, flat_piece, (((0,), (1,)), ((), ())), prefe...  18.9 us
    dot_general x1, matrix products, local(): jnp.einsum('jcr,jcs->crs', centered, centered, precision=highest)  16.8 us
  transfers between devices with their start and end apart: 2, of which 2 were waited for; matrix products, arithmetic and copies ran while one was open for 8% of the time, Pallas kernels for 0%

profile of v2, /device:TPU:0, one launch (start us, length us, event | category | flops | bytes accessed | tf_op | source)
XLA Modules:
  0.0 485.4 jit_solution(14091650747524074656)
XLA Ops:
  7.2 0.0 all-gather.3.cloned.1.call-start
  7.2 0.7 all-gather.3.cloned.1.call-update
  7.9 0.0 all-reduce.6.cloned.1.call-start
  7.9 12.0 %copy.10 = bf16[512,8192]{0,1:T(8,128)(2,1)} copy(bf16[512,8192]{1,0:T(8,128)(2,1)} %param.4) | data formatting | bytes 16777216 | tf_op args[1]
  19.9 12.4 %copy.11 = bf16[512,16,512]{2,0,1:T(8,128)(2,1)} copy(bf16[512,16,512]{0,2,1:T(8,128)(2,1)} %bitcast.36) | data formatting | bytes 16777216 | tf_op jit(solution)/shard_map/all_to_all | solution.py:23
  32.3 113.6 %all_to_all.28 = bf16[512,16,512]{2,0,1:T(8,128)(2,1)} all-to-all(bf16[512,16,512]{2,0,1:T(8,128)(2,1)} %copy.11), channel_id=1, replica_groups=mesh['dp_0'=4,'dp_1'=2,'mp_0'=4,'mp_1'=4] {'mp_0','mp_1'}, dimensions={1} | all-to-all | bytes 16777216 | tf_op jit(solution)/shard_map/all_to_all | solution.py:23
  145.9 101.4 %all-gather.3.cloned.1.call-done = bf16[128,192,512]{2,1,0:T(8,128)(2,1)} async-done(((bf16[8,192,512]{2,1,0:T(8,128)(2,1)}), bf16[128,192,512]{2,1,0:T(8,128)(2,1)}) %all-gather.3.cloned.1.call-update) | async-done | bytes 25165840 | tf_op jit(solution)/shard_map/all_gather | solution.py:24
  247.3 18.9 %fusion.5 = f32[512,8,192]{0,2,1:T(8,128)S(1)} fusion(bf16[16,8,192,512]{3,2,1,0:T(8,128)(2,1)} %bitcast.38, bf16[512,16,512]{2,0,1:T(8,128)(2,1)} %all_to_all.28), kind=kOutput, calls=%fused_computation.10 | convolution fusion | flops 12884901888 | bytes 36700160 | tf_op jit(solution)/shard_map/dot_general | solution.py:26
  266.2 0.0 copy-start
  266.2 1.7 copy-done
  267.9 42.6 %all_to_all.29 = f32[512,8,192]{0,2,1:T(8,128)S(1)} all-to-all(f32[512,8,192]{0,2,1:T(8,128)S(1)} %fusion.5), channel_id=1, replica_groups=mesh['dp_0'=4,'dp_1'=2,'mp_0'=4,'mp_1'=4] {'dp_0','dp_1'}, dimensions={1} | all-to-all | bytes 6291456 | tf_op jit(solution)/shard_map/all_to_all | solution.py:39
  310.5 0.3 reduce_sum.65
  310.8 0.6 multiply_reduce_fusion.1
  311.3 16.8 %fusion.4 = bf16[1,1536,1536]{2,1,0:T(8,128)(2,1)} fusion(f32[512,1536]{0,1:T(8,128)S(1)} %bitcast.37), kind=kOutput, calls=%fused_computation.6 | convolution fusion | flops 14497873920 | bytes 7864320 | tf_op jit(solution)/shard_map/jcr,jcs->crs/dot_general | solution.py:47
  328.1 0.0 copy-start.1
  328.1 0.0 all-reduce.6.cloned.1.call-update
  328.1 0.7 copy-done.1
  328.8 3.9 convolution_bitcast_fusion
  332.7 0.1 slice_bitcast_fusion.1
  332.7 2.0 multiply_reduce_fusion.2
  336.0 5.4 %copy.13 = f32[512,1,1536]{2,1,0:T(1,128)} copy(f32[512,1,1536]{0,2,1:T(8,128)S(1)} %bitcast.35) | data formatting | bytes 6291456
  341.5 0.7 multiply_reduce_fusion.4
  342.1 91.3 %all-reduce.6.cloned.1.call-done = bf16[1,1536,1536]{2,1,0:T(8,128)(2,1)} async-done(((bf16[1,1536,1536]{2,1,0:T(8,128)(2,1)}), bf16[1,1536,1536]{2,1,0:T(8,128)(2,1)}) %all-reduce.6.cloned.1.call-update) | async-done | bytes 4718608 | tf_op jit(solution)/shard_map/psum | solution.py:48
  433.5 5.3 %multiply_reduce_fusion = f32[]{:T(128)} fusion(bf16[1,1536,1536]{2,1,0:T(8,128)(2,1)} %all-reduce.6.cloned.1.call-done), kind=kLoop, calls=%fused_computation.3 | loop fusion | flops 7077887 | bytes 4718596 | tf_op jit(solution)/shard_map/reduce_sum | solution.py:50
  440.0 11.3 %all-reduce.2 = (f32[]{:T(128)}, f32[]{:T(128)}, f32[]{:T(128)}) all-reduce(f32[]{:T(128)S(6)} %add.47, f32[]{:T(128)} %get-tuple-element.11, f32[]{:T(128)S(6)} %sub.61), channel_id=1, replica_groups=mesh['dp_0'=4,'dp_1'=2,'mp_0'=4,'mp_1'=4] {'dp_0'}, use_global_device_ids=true, to_apply=%region_2.0 | all-reduce | flops 3 | bytes 24 | tf_op jit(solution)/shard_map/psum | solution.py:16
  451.3 3.2 all-reduce.3
  454.4 11.0 %all-reduce.1 = (f32[]{:T(128)}, f32[]{:T(128)}, f32[]{:T(128)}) all-reduce(f32[]{:T(128)} %get-tuple-element.21, f32[]{:T(128)} %get-tuple-element.22, f32[]{:T(128)} %get-tuple-element.23), channel_id=1, replica_groups=mesh['dp_0'=4,'dp_1'=2,'mp_0'=4,'mp_1'=4] {'mp_0'}, use_global_device_ids=true, to_apply=%region_4.5 | all-reduce | flops 3 | bytes 24 | tf_op jit(solution)/shard_map/psum | solution.py:16
  465.4 9.4 %all-reduce = (f32[]{:T(128)}, f32[]{:T(128)}, f32[]{:T(128)}) all-reduce(f32[]{:T(128)} %get-tuple-element.15, f32[]{:T(128)} %get-tuple-element.16, f32[]{:T(128)} %get-tuple-element.17), channel_id=1, replica_groups=mesh['dp_0'=4,'dp_1'=2,'mp_0'=4,'mp_1'=4] {'mp_1'}, use_global_device_ids=true, to_apply=%region_5.6 | all-reduce | flops 3 | bytes 24 | tf_op jit(solution)/shard_map/psum | solution.py:16
  478.0 0.6 pad_maximum_fusion
  (1 shorter events, 0.0 us)
Async XLA Ops:
  7.2 240.2 %all-gather.3.cloned.1.call-start = ((), (), s32[]{:S(2)}) async-start(), calls=%async_computation.3 | async-start | bytes 26738688 | tf_op jit(solution)/shard_map/all_gather | solution.py:24
  7.9 425.6 %all-reduce.6.cloned.1.call-start = ((), (), s32[]{:S(2)}) async-start(), calls=%async_computation.2 | async-start | bytes 9437184 | tf_op jit(solution)/shard_map/psum | solution.py:48
  266.2 1.7 copy-start
  328.1 0.7 copy-start.1
Sparse Core Ops, SparseCore 0:
  10.1 237.1 all-gather.2
  328.2 105.1 all-reduce.5
